TPU v7x, 32 devices: a whole 2x2x4 slice. The times are simulated.
32 devices in a mesh: ctx: 8 (over y, x, core), dp: 4 (over z).
Axes of the slice: x: 2, y: 2, z: 4, core: 2. Of those that a mesh axis runs over, the one named last changes fastest.
Arguments:
- query_previous: bfloat16 [4, 1024, 2048], P('dp', 'ctx'), may hold values from -240 to 240
- key_previous: bfloat16 [4, 1024, 512], P('dp', 'ctx'), may hold values from -6 to 6
- value_previous: bfloat16 [4, 1024, 512], P('dp', 'ctx'), may hold values from -6 to 6
- span_order: int32 [16], replicated, may hold values from 0 to 15, each once
- resid: bfloat16 [4, 1024, 4096], P('dp', 'ctx'), may hold values from -6 to 6
- grad_norm: bfloat16 [4, 1024, 4096], P('dp', 'ctx'), may hold values from -3 to 3
- gain: float32 [4096], replicated, may hold values from 0.1 to 1.9
Outputs:
- out_prev: bfloat16 [4, 1024, 2048], P('dp', 'ctx')
- lse_prev: float32 [4, 16, 1024], P('dp', None, 'ctx')
- resid_grad: bfloat16 [4, 1024, 4096], P('dp', 'ctx')
- gain_grad: float32 [4096], replicated
Inputs may be any that keep to these rules, and one draw needn't show every extreme that they name: span_order names each of the 16 spans once; rows c * 64 to (c + 1) * 64 - 1 of a sequence's arrays hold span span_order[c].
All inputs are finite; a program needn't handle non-finite values.
Results may differ from a plain program's by a relative error of at most 0.0055.
Values may be sent and summed in bfloat16 or wider, within the bound.
No kernel may reach another device: no remote copies, remote signals or barrier semaphores. Data moves between devices by JAX's collectives and lax.ppermute only.
A program may use at most 64 MiB of HBM per device.

v0:
```python
import math
import jax
import jax.numpy as jnp
from jax import lax
from jax.sharding import PartitionSpec as P

QUERY_HEADS = 16
KEY_VALUE_HEADS = 4
HEAD_WIDTH = 128


def key_positions(tally_count, span_order, half):
    index = jnp.arange(tally_count, dtype=jnp.int32)
    slot = index // half
    table = slot[:, None] == jnp.arange(span_order.shape[0], dtype=jnp.int32)[None, :]
    chosen = jnp.sum(jnp.where(table, span_order[None, :], 0), axis=1)
    return chosen * half + index % half


def dense_update(query_rows, q_positions, carry, key_rows, value_rows, k_positions):
    top, total, summed = carry
    scores = jnp.einsum(
        "rkgd,skd->kgrs", query_rows, key_rows, preferred_element_type=jnp.float32
    ) * HEAD_WIDTH ** (-0.5)
    mask = (k_positions[None, :] <= q_positions[:, None])[None, None]
    scores = jnp.where(mask, scores, -1e30)
    new_top = jnp.maximum(top, jnp.max(scores, axis=-1))
    weights = jnp.where(mask, jnp.exp(scores - new_top[..., None]), 0.0)
    factor = jnp.exp(top - new_top)
    total = total * factor + jnp.sum(weights, axis=-1)
    probs = weights.astype(jnp.bfloat16)
    added = jnp.einsum("kgrs,skd->rkgd", probs, value_rows, preferred_element_type=jnp.float32)
    summed = summed * jnp.transpose(factor, (2, 0, 1))[..., None] + added
    return (new_top, total, summed)


def update(query_rows, q_positions, carry, key_rows, value_rows, k_positions):
    later = jnp.min(k_positions) > jnp.max(q_positions)
    return lax.cond(
        later,
        lambda state: state,
        lambda state: dense_update(
            query_rows, q_positions, state, key_rows, value_rows, k_positions
        ),
        carry,
    )


def fold_piece(query_rows, q_positions, carry, k_piece, v_piece, span_order, half):
    tally_count = k_piece.shape[1]
    heads = k_piece.shape[2] // HEAD_WIDTH
    key_rows = k_piece[0].reshape(tally_count, heads, HEAD_WIDTH)
    value_rows = v_piece[0].reshape(tally_count, heads, HEAD_WIDTH)
    k_positions = key_positions(tally_count, span_order, half)
    block = math.gcd(tally_count, 512)
    steps = tally_count // block

    def step_fn(state, items):
        return (update(query_rows, q_positions, state, items[0], items[1], items[2]), None)

    carry, unused = lax.scan(
        step_fn,
        carry,
        (
            key_rows.reshape(steps, block, heads, HEAD_WIDTH),
            value_rows.reshape(steps, block, heads, HEAD_WIDTH),
            k_positions.reshape(steps, block),
        ),
    )
    return carry


def blank_state(heads, query_group, row_indices):
    return (
        jnp.full((heads, query_group, row_indices), -1e30, jnp.float32),
        jnp.zeros((heads, query_group, row_indices), jnp.float32),
        jnp.zeros((row_indices, heads, query_group, HEAD_WIDTH), jnp.float32),
    )


def attention(query_previous, key_previous, value_previous, span_order):
    row_indices = query_previous.shape[1]
    half = row_indices // 2
    query_group = QUERY_HEADS // KEY_VALUE_HEADS
    mine = lax.dynamic_slice_in_dim(span_order, 2 * lax.axis_index("ctx"), 2)
    local = jnp.arange(row_indices, dtype=jnp.int32)
    q_positions = jnp.where(local < half, mine[0], mine[1]) * half + local % half
    query_rows = query_previous[0].reshape(row_indices, KEY_VALUE_HEADS, query_group, HEAD_WIDTH)
    top, total, summed = fold_piece(
        query_rows,
        q_positions,
        blank_state(KEY_VALUE_HEADS, query_group, row_indices),
        lax.all_gather(key_previous, "ctx", axis=1, tiled=True),
        lax.all_gather(value_previous, "ctx", axis=1, tiled=True),
        span_order,
        half,
    )
    output = summed / jnp.transpose(total, (2, 0, 1))[..., None]
    out_prev = output.reshape(1, row_indices, QUERY_HEADS * HEAD_WIDTH).astype(jnp.bfloat16)
    lse_prev = (top + jnp.log(total)).reshape(1, QUERY_HEADS, row_indices)
    return (out_prev, lse_prev)


def norm_backward(resid, grad_norm, gain):
    resid_f = resid[0].astype(jnp.float32)
    grad_f = grad_norm[0].astype(jnp.float32)
    inv_rms = 1.0 / jnp.sqrt(jnp.mean(resid_f * resid_f, axis=-1, keepdims=True) + 1e-05)
    normed = resid_f * inv_rms
    partial_grad = jnp.sum(grad_f * normed, axis=0)
    gain_grad = lax.psum(partial_grad, ("ctx", "dp"))
    scaled = gain[None, :] * grad_f
    resid_grad = (
        (scaled - normed * jnp.mean(scaled * normed, axis=-1, keepdims=True)) * inv_rms
    ).astype(jnp.bfloat16)
    return (gain_grad, resid_grad[None])


def per_device(query_previous, key_previous, value_previous, span_order, resid, grad_norm, gain):
    out_prev, lse_prev = attention(query_previous, key_previous, value_previous, span_order)
    gain_grad, resid_grad = norm_backward(resid, grad_norm, gain)
    return (out_prev, lse_prev, resid_grad, gain_grad)


def solution(mesh):
    return jax.shard_map(
        per_device,
        mesh=mesh,
        in_specs=(
            P("dp", "ctx", None),
            P("dp", "ctx", None),
            P("dp", "ctx", None),
            P(),
            P("dp", "ctx", None),
            P("dp", "ctx", None),
            P(),
        ),
        out_specs=(P("dp", "ctx", None), P("dp", None, "ctx"), P("dp", "ctx", None), P()),
        check_vma=False,
    )
```

profile of v0, /device:TPU:1, one launch (start us, length us, event | category | flops | bytes accessed | tf_op | source)
XLA Modules:
  0.0 89.6 jit_solution(13001923617092184318)
XLA Ops:
  8.7 0.7 dynamic_slice.27
  10.0 1.3 %copy.20 = bf16[1,128,2048]{1,2,0:T(8,128)(2,1)S(1)} copy(bf16[1,128,2048]{2,1,0:T(8,128)(2,1)} %param.11) | data formatting | bytes 1048576 | tf_op args[0]
  11.6 0.7 select_reduce_fusion
  12.4 1.5 %fusion.38 = f32[128]{0:T(128)S(1)} fusion(bf16[1,128,4096]{2,1,0:T(8,128)(2,1)} %param.15), kind=kLoop, calls=%fused_computation.45 | loop fusion | flops 1572736 | bytes 1049088 | tf_op jit(solution)/shard_map/reduce_sum | solution.py:107
  13.9 1.9 %fusion.47 = s32[]{:T(128)} fusion(s32[]{:T(128)} %bitcast.11, s32[]{:T(128)} %bitcast.10), kind=kLoop, calls=%fused_computation.69 | loop fusion | flops 1407 | bytes 12 | tf_op jit(solution)/shard_map/while/body/eval_jaxpr/reduce_max | solution.py:38
  15.9 2.4 %fusion.34 = (f32[4096]{0:T(1024)S(1)}, f32[128]{0:T(128)S(1)}) fusion(bf16[1,128,4096]{2,1,0:T(8,128)(2,1)} %param.15, bf16[1,128,4096]{2,1,0:T(8,128)(2,1)} %param.16, f32[128]{0:T(128)S(1)} %add_rsqrt_fusion, f32[4096]{0:T(1024)} %param.17), kind=kLoop, calls=%fused_computation.41 | loop fusion | flops 4190080 | bytes 2130944 | tf_op jit(solution)/shard_map/reduce_sum | solution.py:109
  18.2 42.3 %psum.7 = f32[4096]{0:T(1024)} all-reduce(f32[4096]{0:T(1024)S(1)} %get-tuple-element.291), channel_id=1, replica_groups=mesh['ctx'=8,'dp'=4] {'ctx','dp'}, use_global_device_ids=true, to_apply=%region_12.13 | all-reduce | flops 4096 | bytes 32768 | tf_op jit(solution)/shard_map/psum | solution.py:110
  60.5 1.5 %fusion.37 = bf16[1,128,4096]{2,1,0:T(8,128)(2,1)} fusion(bf16[1,128,4096]{2,1,0:T(8,128)(2,1)S(1)} %copy-done.1, bf16[1,128,4096]{2,1,0:T(8,128)(2,1)S(1)} %copy-done, f32[128]{0:T(128)S(1)} %broadcast_multiply_fusion.1, f32[128]{0:T(128)S(1)} %add_rsqrt_fusion, f32[4096]{0:T(1024)S(1)} %copy-done.3), kind=kLoop, calls=%fused_computation.44 | loop fusion | flops 4194304 | bytes 3163136 | tf_op jit(solution)/shard_map/convert_element_type | solution.py:114
  62.1 1.3 %reshape_reshape_squeeze.6 = bf16[2,512,4,128]{3,2,1,0:T(4,128)(2,1)S(1)} reshape(bf16[1,1024,512]{2,1,0:T(8,128)(2,1)} %all-gather.3.cloned.1.call-done) | data formatting | bytes 2097152 | tf_op jit(solution)/shard_map/reshape;reshape;squeeze | solution.py:65
  63.6 1.3 %reshape_reshape_squeeze.7 = bf16[2,512,4,128]{3,2,1,0:T(4,128)(2,1)S(1)} reshape(bf16[1,1024,512]{2,1,0:T(8,128)(2,1)} %all-gather.5.cloned.1.call-done) | data formatting | bytes 2097152 | tf_op jit(solution)/shard_map/reshape;reshape;squeeze | solution.py:66
  64.9 1.1 %copy.23 = bf16[2,512,4,128]{3,1,2,0:T(8,128)(2,1)} copy(bf16[2,512,4,128]{3,2,1,0:T(4,128)(2,1)S(1)} %reshape_reshape_squeeze.7) | data formatting | bytes 2097152
  66.2 14.0 %while.16 = (s32[]{:T(128)}, f32[4,4,128]{2,1,0:T(4,128)S(1)}, f32[4,4,128]{2,1,0:T(4,128)S(1)}, f32[128,4,4,128]{3,0,2,1:T(8,128)S(1)}, s32[2,512]{1,0:T(2,128)...) while((s32[]{:T(128)}, f32[4,4,128]{2,1,0:T(4,128)S(1)}, ...), condition=%wide.region_8.9_spmd.clone, body=%wide.region_2.8_spmd.clone.sunk | while | flops 551100160 | bytes 20852624 | solution.py:61
  66.2 0.7 fusion.52
  68.2 5.0 %conditional.3 = ((f32[4,4,128]{2,1,0:T(4,128)S(1)}, f32[4,4,128]{2,1,0:T(4,128)S(1)}, f32[128,4,4,128]{3,0,2,1:T(8,128)S(1)})) conditional(s32[]{:T(128)} %convert_element_type.103, (s32[1,512]{1,0:T(1,128)S(1)}, s32[128]{0:T(128)S(1)}, bf16[2,512,4,128]{3,1,2,0:T(8,128)(2,1)S(1)}, s32[]{:T(128)}, bf16[128,4,4,128]{3,0,2,1:T(8,128)(2,1)S(1)}, ...), branch_computations={%region_4.6_spmd.clone, %region_7.7_spmd} | conditional | flops 551099520 | bytes 20846672 | solution.py:39
  68.2 1.3 %fusion.24 = s32[128]{0:T(128)S(1)} fusion(s32[128]{0:T(128)S(1)} %get-tuple-element.268, s32[128]{0:T(128)S(1)} %get-tuple-element.267, s32[128]{0:T(128)S(1)} %get-tuple-element.272, s32[128]{0:T(128)S(1)} %get-tuple-element.272, s32[128]{0:T(128)S(1)} %get-tuple-element.272, s32[128]{0:T(128)S(1)} %get-tuple-element.272, s32[]{:T(128)} %get-tuple-element.273, ...), kind=kLoop, calls=%fused_computation.25 | loop fusion | flops 1152 | bytes 3596 | tf_op jit(solution)/shard_map/add | solution.py:87
  69.7 0.8 fusion.2
  70.4 1.0 %fusion.4 = f32[4,4,128]{2,1,0:T(4,128)S(1)} fusion(f32[4,512,128,4]{2,1,3,0:T(8,128)S(1)} %get-tuple-element.320, f32[4,4,128]{2,1,0:T(4,128)S(1)} %get-tuple-element.400, pred[128,512]{0,1:T(8,128)(4,1)S(1)} %broadcast_compare_fusion), kind=kLoop, calls=%fused_computation.5 | loop fusion | flops 5240832 | bytes 4276224 | tf_op jit(solution)/shard_map/while/body/eval_jaxpr/cond/branch_0_fun/reduce_sum | solution.py:30
  71.5 1.7 %fusion.11 = f32[128,4,4,128]{3,0,2,1:T(8,128)S(1)} fusion(f32[4,512,128,4]{2,1,3,0:T(8,128)S(1)} %get-tuple-element.320, f32[4,4,128]{2,1,0:T(4,128)S(1)} %get-tuple-element.400, pred[128,512]{0,1:T(8,128)(4,1)S(1)} %broadcast_compare_fusion, f32[128,4,4,128]{3,0,2,1:T(8,128)S(1)} %get-tuple-element.261, bf16[2,512,4,128]{3,1,2,0:T(8,128)(2,1)S(1)} %copy-done.2, ...), kind=kOutput, calls=%fused_computation.9 | convolution fusion | flops 274202624 | bytes 6897668 | tf_op jit(solution)/shard_map/while/body/eval_jaxpr/cond/branch_0_fun/kgrs,skd->rkgd/dot_general | solution.py:32
  75.2 5.0 %conditional.3 = ((f32[4,4,128]{2,1,0:T(4,128)S(1)}, f32[4,4,128]{2,1,0:T(4,128)S(1)}, f32[128,4,4,128]{3,0,2,1:T(8,128)S(1)})) conditional(s32[]{:T(128)} %convert_element_type.103, (s32[1,512]{1,0:T(1,128)S(1)}, s32[128]{0:T(128)S(1)}, bf16[2,512,4,128]{3,1,2,0:T(8,128)(2,1)S(1)}, s32[]{:T(128)}, bf16[128,4,4,128]{3,0,2,1:T(8,128)(2,1)S(1)}, ...), branch_computations={%region_4.6_spmd.clone, %region_7.7_spmd} | conditional | flops 551099520 | bytes 20846672 | solution.py:39
  75.3 1.3 %fusion.24 = s32[128]{0:T(128)S(1)} fusion(s32[128]{0:T(128)S(1)} %get-tuple-element.268, s32[128]{0:T(128)S(1)} %get-tuple-element.267, s32[128]{0:T(128)S(1)} %get-tuple-element.272, s32[128]{0:T(128)S(1)} %get-tuple-element.272, s32[128]{0:T(128)S(1)} %get-tuple-element.272, s32[128]{0:T(128)S(1)} %get-tuple-element.272, s32[]{:T(128)} %get-tuple-element.273, ...), kind=kLoop, calls=%fused_computation.25 | loop fusion | flops 1152 | bytes 3596 | tf_op jit(solution)/shard_map/add | solution.py:87
  76.7 0.8 fusion.2
  77.5 1.0 %fusion.4 = f32[4,4,128]{2,1,0:T(4,128)S(1)} fusion(f32[4,512,128,4]{2,1,3,0:T(8,128)S(1)} %get-tuple-element.320, f32[4,4,128]{2,1,0:T(4,128)S(1)} %get-tuple-element.400, pred[128,512]{0,1:T(8,128)(4,1)S(1)} %broadcast_compare_fusion), kind=kLoop, calls=%fused_computation.5 | loop fusion | flops 5240832 | bytes 4276224 | tf_op jit(solution)/shard_map/while/body/eval_jaxpr/cond/branch_0_fun/reduce_sum | solution.py:30
  78.5 1.7 %fusion.11 = f32[128,4,4,128]{3,0,2,1:T(8,128)S(1)} fusion(f32[4,512,128,4]{2,1,3,0:T(8,128)S(1)} %get-tuple-element.320, f32[4,4,128]{2,1,0:T(4,128)S(1)} %get-tuple-element.400, pred[128,512]{0,1:T(8,128)(4,1)S(1)} %broadcast_compare_fusion, f32[128,4,4,128]{3,0,2,1:T(8,128)S(1)} %get-tuple-element.261, bf16[2,512,4,128]{3,1,2,0:T(8,128)(2,1)S(1)} %copy-done.2, ...), kind=kOutput, calls=%fused_computation.9 | convolution fusion | flops 274202624 | bytes 6897668 | tf_op jit(solution)/shard_map/while/body/eval_jaxpr/cond/branch_0_fun/kgrs,skd->rkgd/dot_general | solution.py:32
  81.0 1.2 %convert_element_type.46 = bf16[1,128,2048]{2,1,0:T(8,128)(2,1)} reshape(bf16[128,4,4,128]{3,2,1,0:T(4,128)(2,1)S(1)} %copy.24) | data formatting | bytes 1048576 | tf_op jit(solution)/shard_map/convert_element_type | solution.py:99
  (46 shorter events, 5.1 us)
Async XLA Ops:
  7.2 53.3 %copy-start = (bf16[1,128,4096]{2,1,0:T(8,128)(2,1)S(1)}, bf16[1,128,4096]{2,1,0:T(8,128)(2,1)}, u32[]{:S(2)}) copy-start(bf16[1,128,4096]{2,1,0:T(8,128)(2,1)} %param.15) | copy-start | bytes 3145732
  7.2 53.3 %copy-start.1 = (bf16[1,128,4096]{2,1,0:T(8,128)(2,1)S(1)}, bf16[1,128,4096]{2,1,0:T(8,128)(2,1)}, u32[]{:S(2)}) copy-start(bf16[1,128,4096]{2,1,0:T(8,128)(2,1)} %param.16) | copy-start | bytes 3145732
  7.2 53.3 %copy-start.3 = (f32[4096]{0:T(1024)S(1)}, f32[4096]{0:T(1024)}, u32[]{:S(2)}) copy-start(f32[4096]{0:T(1024)} %param.17) | copy-start | bytes 49156
  7.2 54.9 %all-gather.3.cloned.1.call-start = ((), (), s32[]{:S(2)}) async-start(), calls=%async_computation | async-start | bytes 1179648 | tf_op jit(solution)/shard_map/all_gather | solution.py:93
  7.9 55.6 %all-gather.5.cloned.1.call-start = ((), (), s32[]{:S(2)}) async-start(), calls=%async_computation.1 | async-start | bytes 1179648 | tf_op jit(solution)/shard_map/all_gather | solution.py:94
  69.7 1.8 %copy-start.2 = (bf16[2,512,4,128]{3,1,2,0:T(8,128)(2,1)S(1)}, bf16[2,512,4,128]{3,1,2,0:T(8,128)(2,1)}, u32[]{:S(2)}) copy-start(bf16[2,512,4,128]{3,1,2,0:T(8,128)(2,1)} %get-tuple-element.262) | copy-start | bytes 3145732 | tf_op jit(solution)/shard_map/while/body/eval_jaxpr/cond
  76.7 1.8 %copy-start.2 = (bf16[2,512,4,128]{3,1,2,0:T(8,128)(2,1)S(1)}, bf16[2,512,4,128]{3,1,2,0:T(8,128)(2,1)}, u32[]{:S(2)}) copy-start(bf16[2,512,4,128]{3,1,2,0:T(8,128)(2,1)} %get-tuple-element.262) | copy-start | bytes 3145732 | tf_op jit(solution)/shard_map/while/body/eval_jaxpr/cond
Sparse Core Ops, SparseCore 0:
  9.9 25.9 all-gather.2
  37.7 23.9 all-gather.4
where the time goes:
time: 90.1 us; the launch traced here: 89.6 us
  blocking collectives  42.3 us (47%)
  other arithmetic  15.4 us (17%)
  between operations  14.2 us (16%)
  local copies, waits for them, and re-layouts  8.61 us (10%)
  matrix products  4.87 us (5%)
  loops' own time  2.82 us (3%)
  waiting for transfers between devices  1.4 us (2%)
    psum x1, blocking collectives, norm_backward(): gain_grad = lax.psum(partial_grad, ('ctx', 'dp'))  42.3 us
    dot_general x2, matrix products, dense_update(): jnp.einsum('kgrs,skd->rkgd', probs, value_rows, preferred_element_type=jn...  3.37 us
    unnamed x10, local copies, waits for them, and re-layouts  2.88 us
    another operation x1, loops' own time, fold_piece(): lax.scan(step_fn, carry, (key_rows.reshape(steps, block, heads, HEAD_WIDT...  2.66 us
    add x2, other arithmetic, attention(): jnp.where(local < half, mine[0], mine[1]) * half + local % half  2.54 us
    reduce_sum x1, other arithmetic, norm_backward(): partial_grad = jnp.sum(grad_f * normed, axis=0)  2.36 us
    reduce_sum x2, other arithmetic, dense_update(): total = total * factor + jnp.sum(weights, axis=-1)  2.02 us
    reduce_max x1, other arithmetic, update(): later = jnp.min(k_positions) > jnp.max(q_positions)  1.93 us
  transfers between devices with their start and end apart: 2, of which 0 were waited for; matrix products, arithmetic and copies ran while one was open for 14% of the time, Pallas kernels for 0%

commit v1 on v0

--- a/solution.py
+++ b/solution.py
@@ -7,6 +7,14 @@
 QUERY_HEADS = 16
 KEY_VALUE_HEADS = 4
 HEAD_WIDTH = 128
+
+
+def compute_levels_all(here_x):
+    group_axis = "ctx"
+    across = "dp"
+    for rr in (group_axis, across):
+        here_x = jax.lax.psum(here_x, rr)
+    return here_x
 
 
 def key_positions(tally_count, span_order, half):
@@ -107,7 +115,7 @@
     inv_rms = 1.0 / jnp.sqrt(jnp.mean(resid_f * resid_f, axis=-1, keepdims=True) + 1e-05)
     normed = resid_f * inv_rms
     partial_grad = jnp.sum(grad_f * normed, axis=0)
-    gain_grad = lax.psum(partial_grad, ("ctx", "dp"))
+    gain_grad = compute_levels_all(partial_grad)
     scaled = gain[None, :] * grad_f
     resid_grad = (
         (scaled - normed * jnp.mean(scaled * normed, axis=-1, keepdims=True)) * inv_rms

time: 90.1 us -> 93 us (1.032)
  the two profiles are of different devices: /device:TPU:1 before, /device:TPU:0 now
where the time goes in v1:
time: 93 us; the launch traced here: 92.6 us
  blocking collectives  45.2 us (49%)
  other arithmetic  15.4 us (17%)
  between operations  14.2 us (15%)
  local copies, waits for them, and re-layouts  8.61 us (9%)
  matrix products  4.87 us (5%)
  loops' own time  2.82 us (3%)
  waiting for transfers between devices  1.4 us (2%)
    psum x2, blocking collectives, compute_levels_all(): here_x = jax.lax.psum(here_x, rr)  45.2 us
    dot_general x2, matrix products, dense_update(): jnp.einsum('kgrs,skd->rkgd', probs, value_rows, preferred_element_type=jn...  3.37 us
    unnamed x10, local copies, waits for them, and re-layouts  2.88 us
    another operation x1, loops' own time, fold_piece(): lax.scan(step_fn, carry, (key_rows.reshape(steps, block, heads, HEAD_WIDT...  2.66 us
    add x2, other arithmetic, attention(): jnp.where(local < half, mine[0], mine[1]) * half + local % half  2.54 us
    reduce_sum x1, other arithmetic, norm_backward(): partial_grad = jnp.sum(grad_f * normed, axis=0)  2.36 us
    reduce_sum x2, other arithmetic, dense_update(): total = total * factor + jnp.sum(weights, axis=-1)  2.02 us
    reduce_max x1, other arithmetic, update(): later = jnp.min(k_positions) > jnp.max(q_positions)  1.93 us
  transfers between devices with their start and end apart: 2, of which 0 were waited for; matrix products, arithmetic and copies ran while one was open for 14% of the time, Pallas kernels for 0%

profile of v1, /device:TPU:0, one launch (start us, length us, event | category | flops | bytes accessed | tf_op | source)
XLA Modules:
  0.0 92.6 jit_solution(5314909566116817877)
XLA Ops:
  8.7 0.7 dynamic_slice.27
  10.0 1.3 %copy.20 = bf16[1,128,2048]{1,2,0:T(8,128)(2,1)S(1)} copy(bf16[1,128,2048]{2,1,0:T(8,128)(2,1)} %param.11) | data formatting | bytes 1048576 | tf_op args[0]
  11.6 0.7 select_reduce_fusion
  12.4 1.5 %fusion.38 = f32[128]{0:T(128)S(1)} fusion(bf16[1,128,4096]{2,1,0:T(8,128)(2,1)} %param.15), kind=kLoop, calls=%fused_computation.45 | loop fusion | flops 1572736 | bytes 1049088 | tf_op jit(solution)/shard_map/reduce_sum | solution.py:115
  13.9 1.9 %fusion.47 = s32[]{:T(128)} fusion(s32[]{:T(128)} %bitcast.11, s32[]{:T(128)} %bitcast.10), kind=kLoop, calls=%fused_computation.69 | loop fusion | flops 1407 | bytes 12 | tf_op jit(solution)/shard_map/while/body/eval_jaxpr/reduce_max | solution.py:46
  15.9 2.4 %fusion.34 = (f32[4096]{0:T(1024)S(1)}, f32[128]{0:T(128)S(1)}) fusion(bf16[1,128,4096]{2,1,0:T(8,128)(2,1)} %param.15, bf16[1,128,4096]{2,1,0:T(8,128)(2,1)} %param.16, f32[128]{0:T(128)S(1)} %add_rsqrt_fusion, f32[4096]{0:T(1024)} %param.17), kind=kLoop, calls=%fused_computation.41 | loop fusion | flops 4190080 | bytes 2130944 | tf_op jit(solution)/shard_map/reduce_sum | solution.py:117
  18.2 25.6 %psum.14 = f32[4096]{0:T(1024)S(1)} all-reduce(f32[4096]{0:T(1024)S(1)} %get-tuple-element.291), channel_id=1, replica_groups=mesh['ctx'=8,'dp'=4] {'ctx'}, use_global_device_ids=true, to_apply=%region_12.13 | all-reduce | flops 4096 | bytes 32768 | tf_op jit(solution)/shard_map/psum | solution.py:16
  43.9 19.6 %psum.15 = f32[4096]{0:T(1024)} all-reduce(f32[4096]{0:T(1024)S(1)} %psum.14), channel_id=1, replica_groups=mesh['ctx'=8,'dp'=4] {'dp'}, use_global_device_ids=true, to_apply=%region_13.14 | all-reduce | flops 4096 | bytes 32768 | tf_op jit(solution)/shard_map/psum | solution.py:16
  63.5 1.5 %fusion.37 = bf16[1,128,4096]{2,1,0:T(8,128)(2,1)} fusion(bf16[1,128,4096]{2,1,0:T(8,128)(2,1)S(1)} %copy-done.1, bf16[1,128,4096]{2,1,0:T(8,128)(2,1)S(1)} %copy-done, f32[128]{0:T(128)S(1)} %broadcast_multiply_fusion.1, f32[128]{0:T(128)S(1)} %add_rsqrt_fusion, f32[4096]{0:T(1024)S(1)} %copy-done.3), kind=kLoop, calls=%fused_computation.44 | loop fusion | flops 4194304 | bytes 3163136 | tf_op jit(solution)/shard_map/convert_element_type | solution.py:122
  65.0 1.3 %reshape_reshape_squeeze.6 = bf16[2,512,4,128]{3,2,1,0:T(4,128)(2,1)S(1)} reshape(bf16[1,1024,512]{2,1,0:T(8,128)(2,1)} %all-gather.3.cloned.1.call-done) | data formatting | bytes 2097152 | tf_op jit(solution)/shard_map/reshape;reshape;squeeze | solution.py:73
  66.5 1.3 %reshape_reshape_squeeze.7 = bf16[2,512,4,128]{3,2,1,0:T(4,128)(2,1)S(1)} reshape(bf16[1,1024,512]{2,1,0:T(8,128)(2,1)} %all-gather.5.cloned.1.call-done) | data formatting | bytes 2097152 | tf_op jit(solution)/shard_map/reshape;reshape;squeeze | solution.py:74
  67.9 1.1 %copy.23 = bf16[2,512,4,128]{3,1,2,0:T(8,128)(2,1)} copy(bf16[2,512,4,128]{3,2,1,0:T(4,128)(2,1)S(1)} %reshape_reshape_squeeze.7) | data formatting | bytes 2097152
  69.1 14.0 %while.16 = (s32[]{:T(128)}, f32[4,4,128]{2,1,0:T(4,128)S(1)}, f32[4,4,128]{2,1,0:T(4,128)S(1)}, f32[128,4,4,128]{3,0,2,1:T(8,128)S(1)}, s32[2,512]{1,0:T(2,128)...) while((s32[]{:T(128)}, f32[4,4,128]{2,1,0:T(4,128)S(1)}, ...), condition=%wide.region_8.9_spmd.clone, body=%wide.region_2.8_spmd.clone.sunk | while | flops 551100160 | bytes 20852624 | solution.py:69
  71.2 5.0 %conditional.3 = ((f32[4,4,128]{2,1,0:T(4,128)S(1)}, f32[4,4,128]{2,1,0:T(4,128)S(1)}, f32[128,4,4,128]{3,0,2,1:T(8,128)S(1)})) conditional(s32[]{:T(128)} %convert_element_type.103, (s32[1,512]{1,0:T(1,128)S(1)}, s32[128]{0:T(128)S(1)}, bf16[2,512,4,128]{3,1,2,0:T(8,128)(2,1)S(1)}, s32[]{:T(128)}, bf16[128,4,4,128]{3,0,2,1:T(8,128)(2,1)S(1)}, ...), branch_computations={%region_4.6_spmd.clone, %region_7.7_spmd} | conditional | flops 551099520 | bytes 20846672 | solution.py:47
  71.2 1.3 %fusion.24 = s32[128]{0:T(128)S(1)} fusion(s32[128]{0:T(128)S(1)} %get-tuple-element.268, s32[128]{0:T(128)S(1)} %get-tuple-element.267, s32[128]{0:T(128)S(1)} %get-tuple-element.272, s32[128]{0:T(128)S(1)} %get-tuple-element.272, s32[128]{0:T(128)S(1)} %get-tuple-element.272, s32[128]{0:T(128)S(1)} %get-tuple-element.272, s32[]{:T(128)} %get-tuple-element.273, ...), kind=kLoop, calls=%fused_computation.25 | loop fusion | flops 1152 | bytes 3596 | tf_op jit(solution)/shard_map/add | solution.py:95
  72.6 0.8 fusion.2
  73.4 1.0 %fusion.4 = f32[4,4,128]{2,1,0:T(4,128)S(1)} fusion(f32[4,512,128,4]{2,1,3,0:T(8,128)S(1)} %get-tuple-element.320, f32[4,4,128]{2,1,0:T(4,128)S(1)} %get-tuple-element.400, pred[128,512]{0,1:T(8,128)(4,1)S(1)} %broadcast_compare_fusion), kind=kLoop, calls=%fused_computation.5 | loop fusion | flops 5240832 | bytes 4276224 | tf_op jit(solution)/shard_map/while/body/eval_jaxpr/cond/branch_0_fun/reduce_sum | solution.py:38
  74.4 1.7 %fusion.11 = f32[128,4,4,128]{3,0,2,1:T(8,128)S(1)} fusion(f32[4,512,128,4]{2,1,3,0:T(8,128)S(1)} %get-tuple-element.320, f32[4,4,128]{2,1,0:T(4,128)S(1)} %get-tuple-element.400, pred[128,512]{0,1:T(8,128)(4,1)S(1)} %broadcast_compare_fusion, f32[128,4,4,128]{3,0,2,1:T(8,128)S(1)} %get-tuple-element.261, bf16[2,512,4,128]{3,1,2,0:T(8,128)(2,1)S(1)} %copy-done.2, ...), kind=kOutput, calls=%fused_computation.9 | convolution fusion | flops 274202624 | bytes 6897668 | tf_op jit(solution)/shard_map/while/body/eval_jaxpr/cond/branch_0_fun/kgrs,skd->rkgd/dot_general | solution.py:40
  78.2 5.0 %conditional.3 = ((f32[4,4,128]{2,1,0:T(4,128)S(1)}, f32[4,4,128]{2,1,0:T(4,128)S(1)}, f32[128,4,4,128]{3,0,2,1:T(8,128)S(1)})) conditional(s32[]{:T(128)} %convert_element_type.103, (s32[1,512]{1,0:T(1,128)S(1)}, s32[128]{0:T(128)S(1)}, bf16[2,512,4,128]{3,1,2,0:T(8,128)(2,1)S(1)}, s32[]{:T(128)}, bf16[128,4,4,128]{3,0,2,1:T(8,128)(2,1)S(1)}, ...), branch_computations={%region_4.6_spmd.clone, %region_7.7_spmd} | conditional | flops 551099520 | bytes 20846672 | solution.py:47
  78.2 1.3 %fusion.24 = s32[128]{0:T(128)S(1)} fusion(s32[128]{0:T(128)S(1)} %get-tuple-element.268, s32[128]{0:T(128)S(1)} %get-tuple-element.267, s32[128]{0:T(128)S(1)} %get-tuple-element.272, s32[128]{0:T(128)S(1)} %get-tuple-element.272, s32[128]{0:T(128)S(1)} %get-tuple-element.272, s32[128]{0:T(128)S(1)} %get-tuple-element.272, s32[]{:T(128)} %get-tuple-element.273, ...), kind=kLoop, calls=%fused_computation.25 | loop fusion | flops 1152 | bytes 3596 | tf_op jit(solution)/shard_map/add | solution.py:95
  79.6 0.8 fusion.2
  80.4 1.0 %fusion.4 = f32[4,4,128]{2,1,0:T(4,128)S(1)} fusion(f32[4,512,128,4]{2,1,3,0:T(8,128)S(1)} %get-tuple-element.320, f32[4,4,128]{2,1,0:T(4,128)S(1)} %get-tuple-element.400, pred[128,512]{0,1:T(8,128)(4,1)S(1)} %broadcast_compare_fusion), kind=kLoop, calls=%fused_computation.5 | loop fusion | flops 5240832 | bytes 4276224 | tf_op jit(solution)/shard_map/while/body/eval_jaxpr/cond/branch_0_fun/reduce_sum | solution.py:38
  81.4 1.7 %fusion.11 = f32[128,4,4,128]{3,0,2,1:T(8,128)S(1)} fusion(f32[4,512,128,4]{2,1,3,0:T(8,128)S(1)} %get-tuple-element.320, f32[4,4,128]{2,1,0:T(4,128)S(1)} %get-tuple-element.400, pred[128,512]{0,1:T(8,128)(4,1)S(1)} %broadcast_compare_fusion, f32[128,4,4,128]{3,0,2,1:T(8,128)S(1)} %get-tuple-element.261, bf16[2,512,4,128]{3,1,2,0:T(8,128)(2,1)S(1)} %copy-done.2, ...), kind=kOutput, calls=%fused_computation.9 | convolution fusion | flops 274202624 | bytes 6897668 | tf_op jit(solution)/shard_map/while/body/eval_jaxpr/cond/branch_0_fun/kgrs,skd->rkgd/dot_general | solution.py:40
  83.9 1.2 %convert_element_type.46 = bf16[1,128,2048]{2,1,0:T(8,128)(2,1)} reshape(bf16[128,4,4,128]{3,2,1,0:T(4,128)(2,1)S(1)} %copy.24) | data formatting | bytes 1048576 | tf_op jit(solution)/shard_map/convert_element_type | solution.py:107
  (47 shorter events, 5.8 us)
Async XLA Ops:
  7.2 56.3 %copy-start = (bf16[1,128,4096]{2,1,0:T(8,128)(2,1)S(1)}, bf16[1,128,4096]{2,1,0:T(8,128)(2,1)}, u32[]{:S(2)}) copy-start(bf16[1,128,4096]{2,1,0:T(8,128)(2,1)} %param.15) | copy-start | bytes 3145732
  7.2 56.3 %copy-start.1 = (bf16[1,128,4096]{2,1,0:T(8,128)(2,1)S(1)}, bf16[1,128,4096]{2,1,0:T(8,128)(2,1)}, u32[]{:S(2)}) copy-start(bf16[1,128,4096]{2,1,0:T(8,128)(2,1)} %param.16) | copy-start | bytes 3145732
  7.2 56.3 %copy-start.3 = (f32[4096]{0:T(1024)S(1)}, f32[4096]{0:T(1024)}, u32[]{:S(2)}) copy-start(f32[4096]{0:T(1024)} %param.17) | copy-start | bytes 49156
  7.2 57.8 %all-gather.3.cloned.1.call-start = ((), (), s32[]{:S(2)}) async-start(), calls=%async_computation | async-start | bytes 1179648 | tf_op jit(solution)/shard_map/all_gather | solution.py:101
  7.9 58.6 %all-gather.5.cloned.1.call-start = ((), (), s32[]{:S(2)}) async-start(), calls=%async_computation.1 | async-start | bytes 1179648 | tf_op jit(solution)/shard_map/all_gather | solution.py:102
  72.6 1.8 %copy-start.2 = (bf16[2,512,4,128]{3,1,2,0:T(8,128)(2,1)S(1)}, bf16[2,512,4,128]{3,1,2,0:T(8,128)(2,1)}, u32[]{:S(2)}) copy-start(bf16[2,512,4,128]{3,1,2,0:T(8,128)(2,1)} %get-tuple-element.262) | copy-start | bytes 3145732 | tf_op jit(solution)/shard_map/while/body/eval_jaxpr/cond
  79.6 1.8 %copy-start.2 = (bf16[2,512,4,128]{3,1,2,0:T(8,128)(2,1)S(1)}, bf16[2,512,4,128]{3,1,2,0:T(8,128)(2,1)}, u32[]{:S(2)}) copy-start(bf16[2,512,4,128]{3,1,2,0:T(8,128)(2,1)} %get-tuple-element.262) | copy-start | bytes 3145732 | tf_op jit(solution)/shard_map/while/body/eval_jaxpr/cond
Sparse Core Ops, SparseCore 0:
  9.9 26.1 all-gather.2
  38.0 23.3 all-gather.4
